TPU v7x, 32 devices: a whole 2x2x4 slice. The times are simulated.
32 devices in a mesh: groups: 2 (over x), pts: 8 (over z, y), lm: 2 (over core).
Axes of the slice: x: 2, y: 2, z: 4, core: 2. Of those that a mesh axis runs over, the one named last changes fastest.
Arguments:
- points: float32 [3, 4096], P(None, ('groups', 'pts', 'lm')), parts along dimension 1, may hold values from 0 to 1, as said below
- targets: float32 [32, 4096], P(None, ('groups', 'pts', 'lm')), parts along dimension 1, may hold values from -12 to 12
- order: int32 [4096], P(('groups', 'pts', 'lm')), parts along dimension 0, may hold values from 0 to 2047, as said below
- landmarks: int32 [2048], P('groups'), parts along dimension 0, may hold values from 0 to 2047, as said below
Outputs:
- coefficients: float32 [32, 4096], P(None, ('groups', 'pts', 'lm')), parts along dimension 1
- residual: float32 [32, 4096], P(None, ('groups', 'pts', 'lm')), parts along dimension 1
There are 2 independent parts, one for each index of `groups`. A program takes and returns all parts, laid end to end along the dimension named above; each array names one. Nothing has to cross between parts.
Inputs may be any that keep to these rules, and one draw needn't show every extreme that they name: Each column is a point of the unit cube. Points are stored in Z-order: the 128 points of each aligned block of columns lie in one box of a regular grid, and consecutive blocks follow the Z-order curve through the boxes. `order`: A permutation of 0 to 2047. `landmarks`: 1024 distinct point indices.
All inputs are finite; a program needn't handle non-finite values.
Results may differ from a plain program's by a relative error of at most 0.0003.
Values sent between devices are 32-bit elements; how exact they have to be, the bound alone decides.
No kernel may reach another device: no remote copies, remote signals or barrier semaphores. Data moves between devices by JAX's collectives and lax.ppermute only.
A program may use at most 128 MiB of HBM per device.

v0:
```python
import math
import jax
import jax.numpy as jnp
from jax import lax
from jax.sharding import PartitionSpec as P

ITERS = 2
root_five = 2.23606797749979
signal_var = 0.1
inverse_square_length = 25.0
highest = lax.Precision.HIGHEST


def matern(near, far):
    first = near[0][:, None] - far[0][None, :]
    second = near[1][:, None] - far[1][None, :]
    third = near[2][:, None] - far[2][None, :]
    scaled = (first * first + second * second + third * third) * inverse_square_length
    reach = jnp.sqrt(scaled)
    return signal_var * (1.0 + root_five * reach + 5.0 / 3.0 * scaled) * jnp.exp(-root_five * reach)


def tile_product(near, piece):
    width = piece.shape[1]
    block = math.gcd(width, 512)

    def accumulate(index, total):
        slab = lax.dynamic_slice_in_dim(piece, index * block, block, 1)
        return total + jnp.dot(slab[3:], matern(slab[:3], near), precision=highest)

    empty = jnp.zeros((piece.shape[0] - 3, near.shape[1]), jnp.float32)
    return lax.fori_loop(0, width // block, accumulate, empty)


def landmark_total(vector, cross):
    return lax.psum(jnp.dot(vector, cross, precision=highest), ("pts", "lm"))


def body(points, targets, order, landmarks):
    rows = points.shape[1]
    count = landmarks.shape[0]
    offset = lax.axis_index(("pts", "lm")) * rows
    every = lax.all_gather(targets, ("pts", "lm"), axis=1, tiled=True)
    goal = jnp.take(every, order, axis=1)
    local = landmarks - offset
    inside = (local >= 0) & (local < rows)
    picked = jnp.where(inside[None, :], jnp.take(points, jnp.clip(local, 0, rows - 1), axis=1), 0.0)
    anchors = lax.psum(picked, ("pts", "lm"))
    cross = matern(points, anchors)
    gram = lax.psum(jnp.einsum("ri,rj->ij", cross, cross, precision=highest), ("pts", "lm"))
    inner = matern(anchors, anchors) + jnp.eye(count, dtype=jnp.float32) + gram
    factor = jnp.linalg.cholesky(inner)
    solution = jnp.zeros_like(goal)
    residual = goal
    summed = landmark_total(residual, cross)
    for step in range(ITERS):
        weights = jax.scipy.linalg.cho_solve((factor, True), summed.T)
        scaled_res = residual - jnp.dot(cross, weights, precision=highest).T
        stacked = jnp.concatenate([points, scaled_res], axis=0)
        image = (
            tile_product(points, lax.all_gather(stacked, ("pts", "lm"), axis=1, tiled=True))
            + scaled_res
        )
        current, curvature, lifted = lax.psum(
            (
                jnp.sum(residual * scaled_res, axis=1),
                jnp.sum(scaled_res * image, axis=1),
                jnp.dot(image, cross, precision=highest),
            ),
            ("pts", "lm"),
        )
        if step == 0:
            stride = current / curvature
            direction = scaled_res
            along = image
            along_lift = lifted
        else:
            ratio = current / previous
            stride = current / (curvature - ratio * current / stride)
            direction = scaled_res + ratio[:, None] * direction
            along = image + ratio[:, None] * along
            along_lift = lifted + ratio[:, None] * along_lift
        solution = solution + stride[:, None] * direction
        residual = residual - stride[:, None] * along
        summed = summed - stride[:, None] * along_lift
        previous = current
    return (solution, residual)


def solution(mesh):
    return jax.shard_map(
        body,
        mesh=mesh,
        in_specs=(
            P(None, ("groups", "pts", "lm")),
            P(None, ("groups", "pts", "lm")),
            P(("groups", "pts", "lm")),
            P("groups"),
        ),
        out_specs=(P(None, ("groups", "pts", "lm")), P(None, ("groups", "pts", "lm"))),
        check_vma=False,
    )
```

profile of v0, /device:TPU:0, one launch (start us, length us, event | category | flops | bytes accessed | tf_op | source)
XLA Modules:
  0.0 779.8 jit_solution(6662976577567026140)
XLA Ops:
  11.5 2.8 gather_fusion.1
  14.7 68.3 %psum.56 = f32[3,1024]{0,1:T(8,128)S(1)} all-reduce(f32[3,1024]{0,1:T(8,128)S(1)} %select_bitcast_fusion), channel_id=1, replica_groups=mesh['groups'=2,'pts'=8,'lm'=2] {'pts','lm'}, use_global_device_ids=true, to_apply=%region_0.1 | all-reduce | flops 3072 | bytes 24576 | tf_op jit(solution)/shard_map/psum | solution.py:48
  84.6 21.3 %all_gather.9 = f32[32,2048]{0,1:T(8,128)S(1)} all-gather(f32[32,128]{0,1:T(8,128)S(1)} %copy.11), channel_id=1, replica_groups=mesh['groups'=2,'pts'=8,'lm'=2] {'pts','lm'}, dimensions={1}, use_global_device_ids=true | all-gather | bytes 278528 | tf_op jit(solution)/shard_map/all_gather | solution.py:43
  106.6 6.6 fusion.103
  114.9 112.6 %all-reduce.9.cloned.1.call-done = (f32[1024,1024]{0,1:T(8,128)}, f32[32,1024]{1,0:T(8,128)}) async-done(((f32[1024,1024]{0,1:T(8,128)}, f32[32,1024]{1,0:T(8,128)}), (f32[1024,1024]{0,1:T(8,128)}, f32[32,1024]{1,0:T(8,128)})) %all-reduce.9.cloned.1.call-update) | async-done | bytes 4325392 | tf_op jit(solution)/shard_map/psum | solution.py:50
  227.5 7.6 add_add_fusion
  235.1 5.3 copy.15
  240.5 7.4 fusion.74
  249.8 11.7 %cholesky.223 = f32[128,128]{1,0:T(8,128)S(1)} custom-call(f32[128,128]{1,0:T(8,128)S(1)} %cholesky.580), custom_call_target="Cholesky" | custom-call | tf_op jit(solution)/shard_map/jit(cholesky)/cholesky | solution.py:52
  261.5 2.5 cholesky.255
  264.0 9.8 %custom-call.64 = f32[1,128,128]{1,2,0:T(8,128)S(1)} custom-call(f32[1,128,128]{2,1,0:T(8,128)S(1)} %get-tuple-element.346), custom_call_target="InvertDiagBlocksLowerTriangular" | custom-call | tf_op jit(solution)/shard_map/jit(cholesky)/cholesky | solution.py:52
  273.8 2.4 constant_dynamic-update-slice_fusion.93
  277.8 11.7 %cholesky.244 = f32[128,128]{1,0:T(8,128)S(1)} custom-call(f32[128,128]{1,0:T(8,128)S(1)} %cholesky.584), custom_call_target="Cholesky" | custom-call | tf_op jit(solution)/shard_map/jit(cholesky)/cholesky | solution.py:52
  290.1 10.0 %custom-call.65 = f32[1,128,128]{1,2,0:T(8,128)S(1)} custom-call(f32[1,128,128]{2,1,0:T(8,128)S(1)} %get-tuple-element.343), custom_call_target="InvertDiagBlocksLowerTriangular" | custom-call | tf_op jit(solution)/shard_map/jit(cholesky)/cholesky | solution.py:52
  301.4 2.1 convolution_subtract_fusion.1
  303.5 11.7 %cholesky.468 = f32[128,128]{1,0:T(8,128)S(1)} custom-call(f32[128,128]{1,0:T(8,128)S(1)} %cholesky.589), custom_call_target="Cholesky" | custom-call | tf_op jit(solution)/shard_map/jit(cholesky)/cholesky | solution.py:52
  316.4 9.8 %custom-call.66 = f32[1,128,128]{1,2,0:T(8,128)S(1)} custom-call(f32[1,128,128]{2,1,0:T(8,128)S(1)} %get-tuple-element.340), custom_call_target="InvertDiagBlocksLowerTriangular" | custom-call | tf_op jit(solution)/shard_map/jit(cholesky)/cholesky | solution.py:52
  327.4 2.3 convolution_subtract_fusion.2
  329.8 12.1 %cholesky.487 = f32[128,128]{1,0:T(8,128)S(1)} custom-call(f32[128,128]{1,0:T(8,128)S(1)} %cholesky.594), custom_call_target="Cholesky" | custom-call | tf_op jit(solution)/shard_map/jit(cholesky)/cholesky | solution.py:52
  343.2 9.8 %custom-call.67 = f32[1,128,128]{1,2,0:T(8,128)S(1)} custom-call(f32[1,128,128]{2,1,0:T(8,128)S(1)} %get-tuple-element.337), custom_call_target="InvertDiagBlocksLowerTriangular" | custom-call | tf_op jit(solution)/shard_map/jit(cholesky)/cholesky | solution.py:52
  354.1 2.3 convolution_subtract_fusion.3
  356.4 11.7 %cholesky.506 = f32[128,128]{1,0:T(8,128)S(1)} custom-call(f32[128,128]{1,0:T(8,128)S(1)} %cholesky.599), custom_call_target="Cholesky" | custom-call | tf_op jit(solution)/shard_map/jit(cholesky)/cholesky | solution.py:52
  369.4 9.8 %custom-call.68 = f32[1,128,128]{1,2,0:T(8,128)S(1)} custom-call(f32[1,128,128]{2,1,0:T(8,128)S(1)} %get-tuple-element.334), custom_call_target="InvertDiagBlocksLowerTriangular" | custom-call | tf_op jit(solution)/shard_map/jit(cholesky)/cholesky | solution.py:52
  380.3 2.5 convolution_subtract_fusion.4
  382.8 11.7 %cholesky.526 = f32[128,128]{1,0:T(8,128)S(1)} custom-call(f32[128,128]{1,0:T(8,128)S(1)} %cholesky.604), custom_call_target="Cholesky" | custom-call | tf_op jit(solution)/shard_map/jit(cholesky)/cholesky | solution.py:52
  395.7 9.8 %custom-call.69 = f32[1,128,128]{1,2,0:T(8,128)S(1)} custom-call(f32[1,128,128]{2,1,0:T(8,128)S(1)} %get-tuple-element.331), custom_call_target="InvertDiagBlocksLowerTriangular" | custom-call | tf_op jit(solution)/shard_map/jit(cholesky)/cholesky | solution.py:52
  406.5 2.0 convolution_subtract_fusion.5
  408.5 11.7 %cholesky.546 = f32[128,128]{1,0:T(8,128)S(1)} custom-call(f32[128,128]{1,0:T(8,128)S(1)} %cholesky.609), custom_call_target="Cholesky" | custom-call | tf_op jit(solution)/shard_map/jit(cholesky)/cholesky | solution.py:52
  421.5 10.0 %custom-call.70 = f32[1,128,128]{1,2,0:T(8,128)S(1)} custom-call(f32[1,128,128]{2,1,0:T(8,128)S(1)} %get-tuple-element.328), custom_call_target="InvertDiagBlocksLowerTriangular" | custom-call | tf_op jit(solution)/shard_map/jit(cholesky)/cholesky | solution.py:52
  434.1 11.7 %cholesky.564 = f32[128,128]{1,0:T(8,128)S(1)} custom-call(f32[128,128]{1,0:T(8,128)S(1)} %convolution_subtract_fusion.6), custom_call_target="Cholesky" | custom-call | tf_op jit(solution)/shard_map/jit(cholesky)/cholesky | solution.py:52
  452.8 4.8 select_select_fusion
  457.6 23.0 %while.38 = (s32[]{:T(128)}, f32[1024,1024]{1,0:T(8,128)}, s32[8,2]{0,1:T(2,128)S(1)}, f32[8,128,128]{2,1,0:T(8,128)S(1)}, s32[]{:T(128)}) while((s32[]{:T(128)}, f32[1024,1024]{1,0:T(8,128)}, s32[8,2]{0,1:T(2,128)S(1)}, f32[8,128,128]{2,1,0:T(8,128)S(1)}, s32[]{:T(128)}) %tuple.182), condition=%wide.while_cond, body=%wide.while_body.sunk | while | flops 2 | bytes 131181 | solution.py:57
  458.2 2.3 bitcast_dynamic-update-slice_fusion.2
  461.1 2.3 bitcast_dynamic-update-slice_fusion.2
  464.0 2.3 bitcast_dynamic-update-slice_fusion.2
  466.8 2.3 bitcast_dynamic-update-slice_fusion.2
  469.7 2.3 bitcast_dynamic-update-slice_fusion.2
  472.6 2.3 bitcast_dynamic-update-slice_fusion.2
  475.5 2.3 bitcast_dynamic-update-slice_fusion.2
  478.4 2.2 bitcast_dynamic-update-slice_fusion.2
  480.6 78.8 %custom-call.74 = f32[8,128,128]{1,2,0:T(8,128)S(1)} custom-call(f32[8,128,128]{2,1,0:T(8,128)S(1)} %get-tuple-element.269), custom_call_target="InvertDiagBlocksLowerTriangular" | custom-call | tf_op jit(solution)/shard_map/jit(_cho_solve)/triangular_solve | solution.py:57
  582.0 20.4 %all_gather.10 = f32[35,2048]{1,0:T(8,128)S(1)} all-gather(f32[35,128]{1,0:T(8,128)S(1)} %pad_maximum_fusion.1), channel_id=1, replica_groups=mesh['groups'=2,'pts'=8,'lm'=2] {'pts','lm'}, dimensions={1}, use_global_device_ids=true | all-gather | bytes 304640 | tf_op jit(solution)/shard_map/all_gather | solution.py:61
  602.5 2.7 while.36
  606.9 30.1 %all-reduce.2 = (f32[32]{0:T(128)S(1)}, f32[32]{0:T(128)S(1)}) all-reduce(f32[32]{0:T(128)S(1)} %get-tuple-element.277, f32[32]{0:T(128)S(1)} %get-tuple-element.276), channel_id=1, replica_groups=mesh['groups'=2,'pts'=8,'lm'=2] {'pts','lm'}, use_global_device_ids=true, to_apply=%region_20.22 | all-reduce | flops 64 | bytes 512 | tf_op jit(solution)/shard_map/psum | solution.py:64
  637.0 55.5 %all-reduce.7.cloned.1.call-done = f32[32,1024]{1,0:T(8,128)} async-done(((f32[32,1024]{1,0:T(8,128)}), f32[32,1024]{1,0:T(8,128)}) %all-reduce.7.cloned.1.call-update) | async-done | bytes 131088 | tf_op jit(solution)/shard_map/psum | solution.py:64
  716.1 22.9 %all_gather.11 = f32[35,2048]{1,0:T(8,128)S(1)} all-gather(f32[35,128]{1,0:T(8,128)S(1)} %pad_maximum_fusion), channel_id=1, replica_groups=mesh['groups'=2,'pts'=8,'lm'=2] {'pts','lm'}, dimensions={1}, use_global_device_ids=true | all-gather | bytes 304640 | tf_op jit(solution)/shard_map/all_gather | solution.py:61
  739.0 2.7 while.37
  741.9 29.8 %all-reduce.1 = (f32[32]{0:T(128)S(1)}, f32[32]{0:T(128)S(1)}) all-reduce(f32[32]{0:T(128)S(1)} %get-tuple-element.275, f32[32]{0:T(128)S(1)} %get-tuple-element.274), channel_id=1, replica_groups=mesh['groups'=2,'pts'=8,'lm'=2] {'pts','lm'}, use_global_device_ids=true, to_apply=%region_27.29 | all-reduce | flops 64 | bytes 512 | tf_op jit(solution)/shard_map/psum | solution.py:64
  (213 shorter events, 87.2 us)
Async XLA Ops:
  7.2 220.3 %all-reduce.9.cloned.1.call-start = ((), (), s32[]{:S(2)}) async-start(), calls=%async_computation.1 | async-start | bytes 8650752 | tf_op jit(solution)/shard_map/psum | solution.py:50
  114.9 577.7 %all-reduce.7.cloned.1.call-start = ((), (), s32[]{:S(2)}) async-start(), calls=%async_computation | async-start | bytes 262144 | tf_op jit(solution)/shard_map/psum | solution.py:64
  247.8 1.9 copy-start
  452.8 106.7 %copy-start.1 = (f32[32,1024]{1,0:T(8,128)S(1)}, f32[32,1024]{1,0:T(8,128)}, u32[]{:S(2)}) copy-start(f32[32,1024]{1,0:T(8,128)} %get-tuple-element.307) | copy-start | bytes 393220
  565.1 16.9 %copy-start.2 = (f32[3,128]{1,0:T(4,128)S(1)}, f32[3,128]{1,0:T(4,128)}, u32[]{:S(2)}) copy-start(f32[3,128]{1,0:T(4,128)} %param.10) | copy-start | bytes 4612
Sparse Core Ops, SparseCore 0:
  115.0 112.4 all-reduce.8
  607.0 85.4 all-reduce.6
where the time goes:
time: 789 us; the launch traced here: 780 us
  other arithmetic  276 us (35%)
  blocking collectives  193 us (24%)
  waiting for transfers between devices  168 us (21%)
  matrix products  81.6 us (10%)
  local copies, waits for them, and re-layouts  40.4 us (5%)
  between operations  20.6 us (3%)
    another operation x30, other arithmetic, body(): factor = jnp.linalg.cholesky(inner)  172 us
    psum x1, waiting for transfers between devices, body(): lax.psum(jnp.einsum('ri,rj->ij', cross, cross, precision=highest), ('pts'...  113 us
    another operation x4, other arithmetic, body(): weights = jax.scipy.linalg.cho_solve((factor, True), summed.T)  83.7 us
    psum x1, blocking collectives, body(): anchors = lax.psum(picked, ('pts', 'lm'))  68.3 us
    psum x2, blocking collectives, body(): lax.psum((jnp.sum(residual * scaled_res, axis=1), jnp.sum(scaled_res * im...  59.9 us
    psum x1, waiting for transfers between devices, body(): lax.psum((jnp.sum(residual * scaled_res, axis=1), jnp.sum(scaled_res * im...  55.5 us
    all_gather x2, blocking collectives, body(): lax.all_gather(stacked, ('pts', 'lm'), axis=1, tiled=True)  43.3 us
    another operation x60, matrix products, body(): weights = jax.scipy.linalg.cho_solve((factor, True), summed.T)  41.8 us
  transfers between devices with their start and end apart: 2, of which 2 were waited for; matrix products, arithmetic and copies ran while one was open for 0% of the time, Pallas kernels for 0%

commit v1 on v0

--- a/solution.py
+++ b/solution.py
@@ -47,7 +47,7 @@
     picked = jnp.where(inside[None, :], jnp.take(points, jnp.clip(local, 0, rows - 1), axis=1), 0.0)
     anchors = lax.psum(picked, ("pts", "lm"))
     cross = matern(points, anchors)
-    gram = lax.psum(jnp.einsum("ri,rj->ij", cross, cross, precision=highest), ("pts", "lm"))
+    gram = lax.psum(lax.psum(jnp.einsum("ri,rj->ij", cross, cross, precision=highest), "lm"), "pts")
     inner = matern(anchors, anchors) + jnp.eye(count, dtype=jnp.float32) + gram
     factor = jnp.linalg.cholesky(inner)
     solution = jnp.zeros_like(goal)

time: 789 us -> 841 us (1.066)
  waiting for transfers between devices: 168 us -> 215 us
    psum x1 -> x3, waiting for transfers between devices: 113 us -> 159 us  [the longest x1 133 us: body(): lax.psum(lax.psum(jnp.einsum('ri,rj->ij', cross, cross, precision=highest...]
  transfers between devices with their start and end apart: 2 -> 4, of which waited for: 2 -> 3; matrix products, arithmetic and copies ran while one was open for 0% -> 39% of each run, Pallas kernels for 0% -> 0%
where the time goes in v1:
time: 841 us; the launch traced here: 831 us
  other arithmetic  275 us (33%)
  waiting for transfers between devices  215 us (26%)
  blocking collectives  199 us (24%)
  matrix products  82.3 us (10%)
  local copies, waits for them, and re-layouts  39.7 us (5%)
  between operations  20.3 us (2%)
    another operation x30, other arithmetic, body(): factor = jnp.linalg.cholesky(inner)  172 us
    psum x1, waiting for transfers between devices, body(): lax.psum(lax.psum(jnp.einsum('ri,rj->ij', cross, cross, precision=highest...  133 us
    another operation x4, other arithmetic, body(): weights = jax.scipy.linalg.cho_solve((factor, True), summed.T)  83.6 us
    psum x1, blocking collectives, body(): anchors = lax.psum(picked, ('pts', 'lm'))  68.3 us
    psum x2, blocking collectives, body(): lax.psum((jnp.sum(residual * scaled_res, axis=1), jnp.sum(scaled_res * im...  60 us
    psum x1, waiting for transfers between devices, body(): lax.psum((jnp.sum(residual * scaled_res, axis=1), jnp.sum(scaled_res * im...  55.5 us
    all_gather x2, blocking collectives, body(): lax.all_gather(stacked, ('pts', 'lm'), axis=1, tiled=True)  43 us
    another operation x60, matrix products, body(): weights = jax.scipy.linalg.cho_solve((factor, True), summed.T)  42.5 us
  transfers between devices with their start and end apart: 4, of which 3 were waited for; matrix products, arithmetic and copies ran while one was open for 39% of the time, Pallas kernels for 0%

profile of v1, /device:TPU:0, one launch (start us, length us, event | category | flops | bytes accessed | tf_op | source)
XLA Modules:
  0.0 830.9 jit_solution(11166429473798761403)
XLA Ops:
  10.2 2.8 gather_fusion.1
  13.4 68.3 %psum.63 = f32[3,1024]{0,1:T(8,128)S(1)} all-reduce(f32[3,1024]{0,1:T(8,128)S(1)} %select_bitcast_fusion), channel_id=1, replica_groups=mesh['groups'=2,'pts'=8,'lm'=2] {'pts','lm'}, use_global_device_ids=true, to_apply=%region_0.1 | all-reduce | flops 3072 | bytes 24576 | tf_op jit(solution)/shard_map/psum | solution.py:48
  82.4 6.6 fusion.103
  89.1 25.5 %all-reduce.8.cloned.1.call-done = f32[1024,1024]{0,1:T(8,128)} async-done(((f32[1024,1024]{0,1:T(8,128)}), f32[1024,1024]{0,1:T(8,128)}) %all-reduce.8.cloned.1.call-update) | async-done | bytes 4194320 | tf_op jit(solution)/shard_map/psum | solution.py:50
  114.8 27.9 %all_gather.9 = f32[32,2048]{0,1:T(8,128)S(1)} all-gather(f32[32,128]{0,1:T(8,128)S(1)} %copy.11), channel_id=1, replica_groups=mesh['groups'=2,'pts'=8,'lm'=2] {'pts','lm'}, dimensions={1}, use_global_device_ids=true | all-gather | bytes 278528 | tf_op jit(solution)/shard_map/all_gather | solution.py:43
  145.1 133.4 %all-reduce.10.cloned.1.call-done = f32[1024,1024]{0,1:T(8,128)} async-done(((f32[1024,1024]{0,1:T(8,128)}), f32[1024,1024]{0,1:T(8,128)}) %all-reduce.10.cloned.1.call-update) | async-done | bytes 4194320 | tf_op jit(solution)/shard_map/psum | solution.py:50
  278.5 7.6 add_add_fusion
  286.1 5.4 copy.15
  291.5 7.4 fusion.74
  300.8 11.7 %cholesky.223 = f32[128,128]{1,0:T(8,128)S(1)} custom-call(f32[128,128]{1,0:T(8,128)S(1)} %cholesky.580), custom_call_target="Cholesky" | custom-call | tf_op jit(solution)/shard_map/jit(cholesky)/cholesky | solution.py:52
  312.5 9.8 %custom-call.64 = f32[1,128,128]{1,2,0:T(8,128)S(1)} custom-call(f32[1,128,128]{2,1,0:T(8,128)S(1)} %get-tuple-element.344), custom_call_target="InvertDiagBlocksLowerTriangular" | custom-call | tf_op jit(solution)/shard_map/jit(cholesky)/cholesky | solution.py:52
  322.3 2.5 cholesky.255
  324.8 2.4 constant_dynamic-update-slice_fusion.93
  328.8 11.7 %cholesky.244 = f32[128,128]{1,0:T(8,128)S(1)} custom-call(f32[128,128]{1,0:T(8,128)S(1)} %cholesky.584), custom_call_target="Cholesky" | custom-call | tf_op jit(solution)/shard_map/jit(cholesky)/cholesky | solution.py:52
  341.1 10.0 %custom-call.65 = f32[1,128,128]{1,2,0:T(8,128)S(1)} custom-call(f32[1,128,128]{2,1,0:T(8,128)S(1)} %get-tuple-element.341), custom_call_target="InvertDiagBlocksLowerTriangular" | custom-call | tf_op jit(solution)/shard_map/jit(cholesky)/cholesky | solution.py:52
  352.4 2.1 convolution_subtract_fusion.1
  354.5 11.7 %cholesky.468 = f32[128,128]{1,0:T(8,128)S(1)} custom-call(f32[128,128]{1,0:T(8,128)S(1)} %cholesky.589), custom_call_target="Cholesky" | custom-call | tf_op jit(solution)/shard_map/jit(cholesky)/cholesky | solution.py:52
  367.4 9.8 %custom-call.66 = f32[1,128,128]{1,2,0:T(8,128)S(1)} custom-call(f32[1,128,128]{2,1,0:T(8,128)S(1)} %get-tuple-element.338), custom_call_target="InvertDiagBlocksLowerTriangular" | custom-call | tf_op jit(solution)/shard_map/jit(cholesky)/cholesky | solution.py:52
  378.4 2.3 convolution_subtract_fusion.2
  380.8 12.1 %cholesky.487 = f32[128,128]{1,0:T(8,128)S(1)} custom-call(f32[128,128]{1,0:T(8,128)S(1)} %cholesky.594), custom_call_target="Cholesky" | custom-call | tf_op jit(solution)/shard_map/jit(cholesky)/cholesky | solution.py:52
  394.2 9.8 %custom-call.67 = f32[1,128,128]{1,2,0:T(8,128)S(1)} custom-call(f32[1,128,128]{2,1,0:T(8,128)S(1)} %get-tuple-element.335), custom_call_target="InvertDiagBlocksLowerTriangular" | custom-call | tf_op jit(solution)/shard_map/jit(cholesky)/cholesky | solution.py:52
  405.1 2.3 convolution_subtract_fusion.3
  407.4 11.7 %cholesky.506 = f32[128,128]{1,0:T(8,128)S(1)} custom-call(f32[128,128]{1,0:T(8,128)S(1)} %cholesky.599), custom_call_target="Cholesky" | custom-call | tf_op jit(solution)/shard_map/jit(cholesky)/cholesky | solution.py:52
  420.4 9.8 %custom-call.68 = f32[1,128,128]{1,2,0:T(8,128)S(1)} custom-call(f32[1,128,128]{2,1,0:T(8,128)S(1)} %get-tuple-element.332), custom_call_target="InvertDiagBlocksLowerTriangular" | custom-call | tf_op jit(solution)/shard_map/jit(cholesky)/cholesky | solution.py:52
  431.3 2.5 convolution_subtract_fusion.4
  433.8 11.7 %cholesky.526 = f32[128,128]{1,0:T(8,128)S(1)} custom-call(f32[128,128]{1,0:T(8,128)S(1)} %cholesky.604), custom_call_target="Cholesky" | custom-call | tf_op jit(solution)/shard_map/jit(cholesky)/cholesky | solution.py:52
  446.8 9.8 %custom-call.69 = f32[1,128,128]{1,2,0:T(8,128)S(1)} custom-call(f32[1,128,128]{2,1,0:T(8,128)S(1)} %get-tuple-element.329), custom_call_target="InvertDiagBlocksLowerTriangular" | custom-call | tf_op jit(solution)/shard_map/jit(cholesky)/cholesky | solution.py:52
  459.6 11.7 %cholesky.546 = f32[128,128]{1,0:T(8,128)S(1)} custom-call(f32[128,128]{1,0:T(8,128)S(1)} %cholesky.609), custom_call_target="Cholesky" | custom-call | tf_op jit(solution)/shard_map/jit(cholesky)/cholesky | solution.py:52
  472.5 10.0 %custom-call.70 = f32[1,128,128]{1,2,0:T(8,128)S(1)} custom-call(f32[1,128,128]{2,1,0:T(8,128)S(1)} %get-tuple-element.326), custom_call_target="InvertDiagBlocksLowerTriangular" | custom-call | tf_op jit(solution)/shard_map/jit(cholesky)/cholesky | solution.py:52
  485.1 11.7 %cholesky.564 = f32[128,128]{1,0:T(8,128)S(1)} custom-call(f32[128,128]{1,0:T(8,128)S(1)} %convolution_subtract_fusion.6), custom_call_target="Cholesky" | custom-call | tf_op jit(solution)/shard_map/jit(cholesky)/cholesky | solution.py:52
  503.8 4.8 select_select_fusion
  508.6 23.0 %while.38 = (s32[]{:T(128)}, f32[1024,1024]{1,0:T(8,128)}, s32[8,2]{0,1:T(2,128)S(1)}, f32[8,128,128]{2,1,0:T(8,128)S(1)}, s32[]{:T(128)}) while((s32[]{:T(128)}, f32[1024,1024]{1,0:T(8,128)}, s32[8,2]{0,1:T(2,128)S(1)}, f32[8,128,128]{2,1,0:T(8,128)S(1)}, s32[]{:T(128)}) %tuple.182), condition=%wide.while_cond, body=%wide.while_body.sunk | while | flops 2 | bytes 131181 | solution.py:57
  509.2 2.3 bitcast_dynamic-update-slice_fusion.2
  512.1 2.3 bitcast_dynamic-update-slice_fusion.2
  514.9 2.3 bitcast_dynamic-update-slice_fusion.2
  517.8 2.3 bitcast_dynamic-update-slice_fusion.2
  520.7 2.3 bitcast_dynamic-update-slice_fusion.2
  523.6 2.3 bitcast_dynamic-update-slice_fusion.2
  526.5 2.3 bitcast_dynamic-update-slice_fusion.2
  529.3 2.2 bitcast_dynamic-update-slice_fusion.2
  531.6 78.8 %custom-call.74 = f32[8,128,128]{1,2,0:T(8,128)S(1)} custom-call(f32[8,128,128]{2,1,0:T(8,128)S(1)} %get-tuple-element.269), custom_call_target="InvertDiagBlocksLowerTriangular" | custom-call | tf_op jit(solution)/shard_map/jit(_cho_solve)/triangular_solve | solution.py:57
  633.8 20.1 %all_gather.10 = f32[35,2048]{1,0:T(8,128)S(1)} all-gather(f32[35,128]{1,0:T(8,128)S(1)} %pad_maximum_fusion.1), channel_id=1, replica_groups=mesh['groups'=2,'pts'=8,'lm'=2] {'pts','lm'}, dimensions={1}, use_global_device_ids=true | all-gather | bytes 304640 | tf_op jit(solution)/shard_map/all_gather | solution.py:61
  653.9 2.7 while.36
  658.4 30.1 %all-reduce.2 = (f32[32]{0:T(128)S(1)}, f32[32]{0:T(128)S(1)}) all-reduce(f32[32]{0:T(128)S(1)} %get-tuple-element.277, f32[32]{0:T(128)S(1)} %get-tuple-element.276), channel_id=1, replica_groups=mesh['groups'=2,'pts'=8,'lm'=2] {'pts','lm'}, use_global_device_ids=true, to_apply=%region_21.23 | all-reduce | flops 64 | bytes 512 | tf_op jit(solution)/shard_map/psum | solution.py:64
  688.5 55.5 %all-reduce.14.cloned.1.call-done = f32[32,1024]{1,0:T(8,128)} async-done(((f32[32,1024]{1,0:T(8,128)}), f32[32,1024]{1,0:T(8,128)}) %all-reduce.14.cloned.1.call-update) | async-done | bytes 131088 | tf_op jit(solution)/shard_map/psum | solution.py:64
  767.6 22.9 %all_gather.11 = f32[35,2048]{1,0:T(8,128)S(1)} all-gather(f32[35,128]{1,0:T(8,128)S(1)} %pad_maximum_fusion), channel_id=1, replica_groups=mesh['groups'=2,'pts'=8,'lm'=2] {'pts','lm'}, dimensions={1}, use_global_device_ids=true | all-gather | bytes 304640 | tf_op jit(solution)/shard_map/all_gather | solution.py:61
  790.4 2.7 while.37
  793.3 29.8 %all-reduce.1 = (f32[32]{0:T(128)S(1)}, f32[32]{0:T(128)S(1)}) all-reduce(f32[32]{0:T(128)S(1)} %get-tuple-element.275, f32[32]{0:T(128)S(1)} %get-tuple-element.274), channel_id=1, replica_groups=mesh['groups'=2,'pts'=8,'lm'=2] {'pts','lm'}, use_global_device_ids=true, to_apply=%region_28.30 | all-reduce | flops 64 | bytes 512 | tf_op jit(solution)/shard_map/psum | solution.py:64
  (223 shorter events, 88.1 us)
Async XLA Ops:
  7.2 107.4 %all-reduce.8.cloned.1.call-start = ((), (), s32[]{:S(2)}) async-start(), calls=%async_computation | async-start | bytes 8388608 | tf_op jit(solution)/shard_map/psum | solution.py:50
  89.0 25.6 %copy-start.3 = (f32[32,128]{1,0:T(8,128)S(1)}, f32[32,128]{1,0:T(8,128)}, u32[]{:S(2)}) copy-start(f32[32,128]{1,0:T(8,128)} %param.11) | copy-start | bytes 49156
  89.0 25.7 %copy-start.4 = (s32[128]{0:T(128)S(1)}, s32[128]{0:T(128)}, u32[]{:S(2)}) copy-start(s32[128]{0:T(128)} %param.12) | copy-start | bytes 1540
  89.1 189.4 %all-reduce.10.cloned.1.call-start = ((), (), s32[]{:S(2)}) async-start(), calls=%async_computation.1 | async-start | bytes 8388608 | tf_op jit(solution)/shard_map/psum | solution.py:50
  114.6 495.8 %all-reduce.12.cloned.1.call-start = ((), (), s32[]{:S(2)}) async-start(), calls=%async_computation.2 | async-start | bytes 262144 | tf_op jit(solution)/shard_map/psum | solution.py:36
  145.0 599.0 %all-reduce.14.cloned.1.call-start = ((), (), s32[]{:S(2)}) async-start(), calls=%async_computation.3 | async-start | bytes 262144 | tf_op jit(solution)/shard_map/psum | solution.py:64
  298.8 1.9 copy-start
  616.8 16.9 %copy-start.2 = (f32[3,128]{1,0:T(4,128)S(1)}, f32[3,128]{1,0:T(4,128)}, u32[]{:S(2)}) copy-start(f32[3,128]{1,0:T(4,128)} %param.10) | copy-start | bytes 4612
  653.9 90.1 %copy-start.1 = (f32[32,1024]{1,0:T(8,128)S(1)}, f32[32,1024]{1,0:T(8,128)}, u32[]{:S(2)}) copy-start(f32[32,1024]{1,0:T(8,128)} %all-reduce.12.cloned.1.call-done) | copy-start | bytes 393220
Sparse Core Ops, SparseCore 0:
  89.2 25.3 all-reduce.7
  118.3 160.1 all-reduce.9
  282.0 87.8 all-reduce.11
  658.5 85.4 all-reduce.13
